TPU v7x, 32 devices: a whole 2x2x4 slice. The times are simulated.
32 devices in a mesh: mem: 4 (over z), state: 8 (over y, x, core).
Axes of the slice: x: 2, y: 2, z: 4, core: 2. Of those that a mesh axis runs over, the one named last changes fastest.
Arguments:
- anomalies: bfloat16 [64, 32, 32768], P('mem', None, 'state'), may hold values from -0.75 to 0.75
- alpha: bfloat16 [64, 32, 2048], P('mem', None, 'state'), may hold values from -6 to 6
- basis: bfloat16 [2048, 32768], P(None, 'state'), may hold values from -0.1875 to 0.1875
- gradient: bfloat16 [32, 32768], P(None, 'state'), may hold values from -6 to 6
- vertical_root: float32 [32, 32], replicated, may hold values from -1 to 1
- band_gain: float32 [16], replicated, may hold values from 0.25 to 2
- band: int32 [2048], P('state'), may hold values from 0 to 15
- order: int32 [64], replicated, may hold values from 0 to 63, each once
Outputs:
- increment: float32 [32, 32768], P(None, 'state')
- alpha_grad: float32 [64, 32, 2048], P('mem', None, 'state')
Inputs may be any that keep to these rules, and one draw needn't show every extreme that they name: `order`: a permutation: every member is named by exactly one slot.
All inputs are finite; a program needn't handle non-finite values.
Results may differ from a plain program's by a relative error of at most 0.0029.
Values may be sent and summed in bfloat16 or wider, within the bound.
A program may use at most 128 MiB of HBM per device.

v0:
```python
import jax
import jax.numpy as jnp
from jax import lax
from jax.sharding import PartitionSpec as P


def on_device(anomalies, alpha, basis, gradient, vertical_root, band_gain, band, order):
    high = lax.Precision.HIGHEST
    mem_count = lax.axis_size("mem")
    mem_rank = lax.axis_index("mem")
    member_dev, levels, columns = anomalies.shape
    mode_rows = alpha.shape[2]
    bands = band_gain.shape[0]
    onehot = (band[:, None] == jnp.arange(bands, dtype=jnp.int32)[None, :]).astype(jnp.float32)
    filter_gain = jnp.sum(onehot * band_gain[None, :], axis=1)
    coef = jnp.einsum("ab,jbk->jak", vertical_root, alpha.astype(jnp.float32), precision=high)
    coef = (coef * filter_gain[None, None, :]).astype(jnp.bfloat16)
    members = mem_rank * member_dev + jnp.arange(member_dev, dtype=jnp.int32)
    select = (order[None, :] == members[:, None]).astype(jnp.bfloat16)
    state_count = lax.axis_size("state")
    gathered = lax.all_gather(coef[None], ("mem", "state"), axis=0, tiled=True)
    blocks = gathered.reshape(mem_count, state_count, member_dev, levels, mode_rows)
    picked = jnp.einsum(
        "imj,msjlc->ilsc",
        select.reshape(member_dev, mem_count, member_dev),
        blocks,
        preferred_element_type=jnp.float32,
    )
    picked = picked.astype(jnp.bfloat16).reshape(member_dev * levels, state_count * mode_rows)
    member_field = jnp.dot(picked, basis, preferred_element_type=jnp.float32)
    partial_value = jnp.sum(
        anomalies.astype(jnp.float32) * member_field.reshape(member_dev, levels, columns), axis=0
    )
    increment = lax.psum(partial_value, "mem")
    weighted = (anomalies.astype(jnp.float32) * gradient.astype(jnp.float32)[None]).astype(
        jnp.bfloat16
    )
    weighted = weighted.reshape(member_dev * levels, columns)
    projected = lax.psum_scatter(
        lax.dot_general(
            basis, weighted, (((1,), (1,)), ((), ())), preferred_element_type=jnp.float32
        ),
        "state",
        scatter_dimension=0,
        tiled=True,
    )
    member_grad = jnp.einsum(
        "ab,kma->mbk",
        vertical_root,
        projected.reshape(mode_rows, member_dev, levels),
        precision=high,
    )
    member_grad = member_grad * filter_gain[None, None, :]
    placed = jnp.einsum("ij,ibk->jbk", select.astype(jnp.float32), member_grad, precision=high)
    outgoing = placed.reshape(mem_count, member_dev, levels, mode_rows)
    incoming = lax.all_to_all(outgoing, "mem", split_axis=0, concat_axis=0, tiled=True)
    alpha_grad = jnp.sum(incoming, axis=0)
    return (increment, alpha_grad)


def solution(mesh):
    return jax.shard_map(
        on_device,
        mesh=mesh,
        in_specs=(
            P("mem", None, "state"),
            P("mem", None, "state"),
            P(None, "state"),
            P(None, "state"),
            P(),
            P(),
            P("state"),
            P(),
        ),
        out_specs=(P(None, "state"), P("mem", None, "state")),
        check_vma=False,
    )
```

profile of v0, /device:TPU:0, one launch (start us, length us, event | category | flops | bytes accessed | tf_op | source)
XLA Modules:
  0.0 206.5 jit_solution(10233362292895392196)
XLA Ops:
  8.0 0.0 copy-start
  8.0 0.0 reduce-scatter.2.cloned.1.call-start
  8.1 1.0 convert_element_type.31
  9.1 3.3 %fusion.3 = bf16[16,32,4096]{2,1,0:T(8,128)(2,1)S(1)} fusion(bf16[16,32,4096]{2,1,0:T(8,128)(2,1)} %param.8, f32[32,4096]{1,0:T(8,128)S(1)} %convert_element_type.31), kind=kLoop, calls=%fused_computation.5 | loop fusion | flops 6291456 | bytes 8912896 | tf_op jit(solution)/shard_map/convert_element_type | solution.py:35
  12.4 13.7 %convolution_bitcast_fusion = f32[2048,512]{0,1:T(8,128)} fusion(bf16[512,4096]{1,0:T(8,128)(2,1)S(1)} %bitcast.44, bf16[2048,4096]{1,0:T(8,128)(2,1)} %param.10), kind=kOutput, calls=%fused_computation.9 | convolution fusion | flops 8589934592 | bytes 25165824 | tf_op jit(solution)/shard_map/dot_general | solution.py:40
  26.2 0.0 copy-start.3
  26.2 0.0 copy-start.4
  26.2 0.0 copy-start.1
  26.2 0.0 copy-start.2
  26.2 0.0 reduce-scatter.2.cloned.1.call-update
  26.2 0.0 all-gather.3.cloned.1.call-start
  26.2 0.6 copy-done.3
  26.8 0.0 copy-done.4
  26.8 0.1 select_reduce_fusion
  26.9 0.0 copy-done
  26.9 0.0 copy-done.1
  26.9 1.1 fusion.15
  28.0 0.0 all-gather.3.cloned.1.call-update
  28.0 0.0 copy-done.2
  28.0 0.1 eq.38
  28.1 52.4 %reduce-scatter.2.cloned.1.call-done = f32[256,512]{0,1:T(8,128)} async-done(((f32[2048,512]{0,1:T(8,128)}), f32[256,512]{0,1:T(8,128)}) %reduce-scatter.2.cloned.1.call-update) | async-done | bytes 524304 | tf_op jit(solution)/shard_map/reduce_scatter | solution.py:39
  80.5 1.7 fusion.13
  82.2 1.2 fusion.16
  83.3 1.6 copy.30
  84.9 4.6 %all-to-all-start = ((f32[4,16,32,256]{3,1,2,0:T(8,128)}), f32[4,16,32,256]{3,1,2,0:T(8,128)S(1)}, u32[]{:S(2)}, u32[]{:S(2)}) async-start(f32[4,16,32,256]{3,1,2,0:T(8,128)} %copy.30), calls=%async_computation.1 | async-start | bytes 4194304 | tf_op jit(solution)/shard_map/all_to_all | solution.py:56
  89.5 0.0 all-reduce.2.cloned.1.call-start
  89.5 41.0 %all-gather.3.cloned.1.call-done = bf16[512,32,256]{2,1,0:T(8,128)(2,1)} async-done(((bf16[16,32,256]{2,1,0:T(8,128)(2,1)}), bf16[512,32,256]{2,1,0:T(8,128)(2,1)}) %all-gather.3.cloned.1.call-update) | async-done | bytes 8388624 | tf_op jit(solution)/shard_map/all_gather | solution.py:21
  130.5 8.1 %fusion.10 = bf16[16,32,8,256]{3,0,1,2:T(8,128)(2,1)S(1)} fusion(bf16[4,8,16,32,256]{4,3,2,1,0:T(8,128)(2,1)} %bitcast.46, s32[4,16]{1,0:T(4,128)S(1)} %eq.38, s32[16]{0:T(128)S(1)} %iota_add_fusion), kind=kOutput, calls=%fused_computation.10 | convolution fusion | flops 135267328 | bytes 10486080 | tf_op jit(solution)/shard_map/imj,msjlc->ilsc/dot_general | solution.py:23
  138.6 2.5 %copy.27 = bf16[16,32,8,256]{3,2,1,0:T(8,128)(2,1)} copy(bf16[16,32,8,256]{3,0,1,2:T(8,128)(2,1)S(1)} %fusion.10) | data formatting | bytes 4194304 | tf_op jit(solution)/shard_map/convert_element_type | solution.py:29
  141.1 4.2 %dot_general.24 = bf16[16,32,2048]{2,1,0:T(8,128)(2,1)} reshape(bf16[16,32,8,256]{3,2,1,0:T(8,128)(2,1)} %copy.27) | data formatting | bytes 4194304 | tf_op jit(solution)/shard_map/dot_general | solution.py:30
  145.3 14.4 %fusion.2 = f32[32,4096]{1,0:T(8,128)} fusion(bf16[16,32,4096]{2,1,0:T(8,128)(2,1)} %param.8, bf16[16,32,2048]{2,1,0:T(8,128)(2,1)} %dot_general.24, bf16[2048,4096]{1,0:T(8,128)(2,1)} %param.10), kind=kOutput, calls=%fused_computation.4 | convolution fusion | flops 8596094976 | bytes 23592960 | tf_op jit(solution)/shard_map/dot_general | solution.py:30
  159.8 0.0 all-reduce.2.cloned.1.call-update
  159.8 0.0 all-to-all-done
  159.8 0.2 reduce_sum.29
  160.1 1.1 copy.32
  161.2 36.1 %all-reduce.2.cloned.1.call-done = f32[32,4096]{1,0:T(8,128)} async-done(((f32[32,4096]{1,0:T(8,128)}), f32[32,4096]{1,0:T(8,128)}) %all-reduce.2.cloned.1.call-update) | async-done | bytes 524304 | tf_op jit(solution)/shard_map/psum | solution.py:34
  197.2 1.9 copy.47
  (1 shorter events, 0.0 us)
Async XLA Ops:
  8.0 18.9 %copy-start = (bf16[16,32,256]{2,1,0:T(8,128)(2,1)S(1)}, bf16[16,32,256]{2,1,0:T(8,128)(2,1)}, u32[]{:S(2)}) copy-start(bf16[16,32,256]{2,1,0:T(8,128)(2,1)} %param.9) | copy-start | bytes 786436
  8.0 72.5 %reduce-scatter.2.cloned.1.call-start = ((), (), s32[]{:S(2)}) async-start(), calls=%async_computation.3 | async-start | bytes 4718592 | tf_op jit(solution)/shard_map/reduce_scatter | solution.py:39
  26.2 0.7 copy-start.3
  26.2 0.7 copy-start.4
  26.2 0.8 copy-start.1
  26.2 1.9 copy-start.2
  26.2 104.3 %all-gather.3.cloned.1.call-start = ((), (), s32[]{:S(2)}) async-start(), calls=%async_computation.4 | async-start | bytes 8650752 | tf_op jit(solution)/shard_map/all_gather | solution.py:21
  84.9 74.9 %all-to-all-start = ((f32[4,16,32,256]{3,1,2,0:T(8,128)}), f32[4,16,32,256]{3,1,2,0:T(8,128)S(1)}, u32[]{:S(2)}, u32[]{:S(2)}) async-start(f32[4,16,32,256]{3,1,2,0:T(8,128)} %copy.30), calls=%async_computation.1 | async-start | bytes 4194304 | tf_op jit(solution)/shard_map/all_to_all | solution.py:56
  89.5 107.7 %all-reduce.2.cloned.1.call-start = ((), (), s32[]{:S(2)}) async-start(), calls=%async_computation.2 | async-start | bytes 1048576 | tf_op jit(solution)/shard_map/psum | solution.py:34
Sparse Core Ops, SparseCore 0:
  26.3 54.1 reduce-scatter.1
Sparse Core Ops, SparseCore 1:
  30.1 100.3 all-gather.2
  159.9 37.3 all-reduce.1
where the time goes:
time: 207 us
  waiting for transfers between devices  129 us (62%)
  matrix products  40.2 us (19%)
  between operations  15.6 us (8%)
  local copies, waits for them, and re-layouts  11.9 us (6%)
  starting transfers between devices  4.71 us (2%)
  other arithmetic  4.69 us (2%)
    reduce_scatter x1, waiting for transfers between devices, on_device(): lax.psum_scatter(lax.dot_general(basis, weighted, (((1,), (1,)), ((), ())...  52.4 us
    all_gather x1, waiting for transfers between devices, on_device(): gathered = lax.all_gather(coef[None], ('mem', 'state'), axis=0, tiled=True)  41 us
    psum x1, waiting for transfers between devices, on_device(): increment = lax.psum(partial_value, 'mem')  36.1 us
    dot_general x1, matrix products, on_device(): member_field = jnp.dot(picked, basis, preferred_element_type=jnp.float32)  14.4 us
    dot_general x1, matrix products, on_device(): lax.dot_general(basis, weighted, (((1,), (1,)), ((), ())), preferred_elem...  13.7 us
    dot_general x1, matrix products, on_device(): jnp.einsum('imj,msjlc->ilsc', select.reshape(member_dev, mem_count, membe...  8.11 us
    all_to_all x1, starting transfers between devices, on_device(): lax.all_to_all(outgoing, 'mem', split_axis=0, concat_axis=0, tiled=True)  4.62 us
    dot_general x1, local copies, waits for them, and re-layouts, on_device(): member_field = jnp.dot(picked, basis, preferred_element_type=jnp.float32)  4.19 us
  transfers between devices with their start and end apart: 4, of which 3 were waited for; matrix products, arithmetic and copies ran while one was open for 18% of the time, Pallas kernels for 0%

commit v1 on v0

--- a/solution.py
+++ b/solution.py
@@ -31,7 +31,7 @@
     partial_value = jnp.sum(
         anomalies.astype(jnp.float32) * member_field.reshape(member_dev, levels, columns), axis=0
     )
-    increment = lax.psum(partial_value, "mem")
+    increment = jnp.sum(lax.all_gather(partial_value, "mem"), axis=0)
     weighted = (anomalies.astype(jnp.float32) * gradient.astype(jnp.float32)[None]).astype(
         jnp.bfloat16
     )

time: 207 us -> 214 us (1.034)
  waiting for transfers between devices: 129 us -> 136 us
  other arithmetic: 4.69 us -> 7.23 us
    all_gather x0 -> x1, waiting for transfers between devices: none -> 42.8 us  [on_device(): increment = jnp.sum(lax.all_gather(partial_value, 'mem'), axis=0)]
    psum x1 -> x0, waiting for transfers between devices: 36.1 us -> none  [on_device(): increment = lax.psum(partial_value, 'mem')]
    reduce_sum x0 -> x1, other arithmetic: none -> 2.55 us  [on_device(): increment = jnp.sum(lax.all_gather(partial_value, 'mem'), axis=0)]
  transfers between devices with their start and end apart: 4 -> 4, of which waited for: 3 -> 3; matrix products, arithmetic and copies ran while one was open for 18% -> 17% of each run, Pallas kernels for 0% -> 0%
where the time goes in v1:
time: 214 us
  waiting for transfers between devices  136 us (64%)
  matrix products  40.2 us (19%)
  between operations  15.6 us (7%)
  local copies, waits for them, and re-layouts  10.1 us (5%)
  other arithmetic  7.23 us (3%)
  starting transfers between devices  4.71 us (2%)
    reduce_scatter x1, waiting for transfers between devices, on_device(): lax.psum_scatter(lax.dot_general(basis, weighted, (((1,), (1,)), ((), ())...  52.4 us
    all_gather x1, waiting for transfers between devices, on_device(): increment = jnp.sum(lax.all_gather(partial_value, 'mem'), axis=0)  42.8 us
    all_gather x1, waiting for transfers between devices, on_device(): gathered = lax.all_gather(coef[None], ('mem', 'state'), axis=0, tiled=True)  41 us
    dot_general x1, matrix products, on_device(): member_field = jnp.dot(picked, basis, preferred_element_type=jnp.float32)  14.4 us
    dot_general x1, matrix products, on_device(): lax.dot_general(basis, weighted, (((1,), (1,)), ((), ())), preferred_elem...  13.7 us
    dot_general x1, matrix products, on_device(): jnp.einsum('imj,msjlc->ilsc', select.reshape(member_dev, mem_count, membe...  8.11 us
    all_to_all x1, starting transfers between devices, on_device(): lax.all_to_all(outgoing, 'mem', split_axis=0, concat_axis=0, tiled=True)  4.62 us
  transfers between devices with their start and end apart: 4, of which 3 were waited for; matrix products, arithmetic and copies ran while one was open for 17% of the time, Pallas kernels for 0%

profile of v1, /device:TPU:0, one launch (start us, length us, event | category | flops | bytes accessed | tf_op | source)
XLA Modules:
  0.0 213.9 jit_solution(15006399671041799905)
XLA Ops:
  8.0 0.0 copy-start
  8.0 0.0 reduce-scatter.2.cloned.1.call-start
  8.1 1.0 convert_element_type.31
  9.1 3.3 %fusion.3 = bf16[16,32,4096]{2,1,0:T(8,128)(2,1)S(1)} fusion(bf16[16,32,4096]{2,1,0:T(8,128)(2,1)} %param.8, f32[32,4096]{1,0:T(8,128)S(1)} %convert_element_type.31), kind=kLoop, calls=%fused_computation.5 | loop fusion | flops 6291456 | bytes 8912896 | tf_op jit(solution)/shard_map/convert_element_type | solution.py:35
  12.4 13.7 %convolution_bitcast_fusion = f32[2048,512]{0,1:T(8,128)} fusion(bf16[512,4096]{1,0:T(8,128)(2,1)S(1)} %bitcast.45, bf16[2048,4096]{1,0:T(8,128)(2,1)} %param.10), kind=kOutput, calls=%fused_computation.9 | convolution fusion | flops 8589934592 | bytes 25165824 | tf_op jit(solution)/shard_map/dot_general | solution.py:40
  26.2 0.0 copy-start.3
  26.2 0.0 copy-start.4
  26.2 0.0 copy-start.1
  26.2 0.0 copy-start.2
  26.2 0.0 reduce-scatter.2.cloned.1.call-update
  26.2 0.0 all-gather.5.cloned.1.call-start
  26.2 0.6 copy-done.3
  26.8 0.0 copy-done.4
  26.8 0.1 select_reduce_fusion
  26.9 0.0 copy-done
  26.9 0.0 copy-done.1
  26.9 1.1 fusion.15
  28.0 0.0 all-gather.5.cloned.1.call-update
  28.0 0.0 copy-done.2
  28.0 0.1 eq.38
  28.1 52.4 %reduce-scatter.2.cloned.1.call-done = f32[256,512]{0,1:T(8,128)} async-done(((f32[2048,512]{0,1:T(8,128)}), f32[256,512]{0,1:T(8,128)}) %reduce-scatter.2.cloned.1.call-update) | async-done | bytes 524304 | tf_op jit(solution)/shard_map/reduce_scatter | solution.py:39
  80.5 1.7 fusion.13
  82.2 1.2 fusion.16
  83.3 1.6 copy.30
  84.9 4.6 %all-to-all-start = ((f32[4,16,32,256]{3,1,2,0:T(8,128)}), f32[4,16,32,256]{3,1,2,0:T(8,128)S(1)}, u32[]{:S(2)}, u32[]{:S(2)}) async-start(f32[4,16,32,256]{3,1,2,0:T(8,128)} %copy.30), calls=%async_computation.1 | async-start | bytes 4194304 | tf_op jit(solution)/shard_map/all_to_all | solution.py:56
  89.5 0.0 all-gather.7.cloned.1.call-start
  89.5 41.0 %all-gather.5.cloned.1.call-done = bf16[512,32,256]{2,1,0:T(8,128)(2,1)} async-done(((bf16[16,32,256]{2,1,0:T(8,128)(2,1)}), bf16[512,32,256]{2,1,0:T(8,128)(2,1)}) %all-gather.5.cloned.1.call-update) | async-done | bytes 8388624 | tf_op jit(solution)/shard_map/all_gather | solution.py:21
  130.5 8.1 %fusion.10 = bf16[16,32,8,256]{3,0,1,2:T(8,128)(2,1)S(1)} fusion(bf16[4,8,16,32,256]{4,3,2,1,0:T(8,128)(2,1)} %bitcast.48, s32[4,16]{1,0:T(4,128)S(1)} %eq.38, s32[16]{0:T(128)S(1)} %iota_add_fusion), kind=kOutput, calls=%fused_computation.10 | convolution fusion | flops 135267328 | bytes 10486080 | tf_op jit(solution)/shard_map/imj,msjlc->ilsc/dot_general | solution.py:23
  138.6 2.5 %copy.27 = bf16[16,32,8,256]{3,2,1,0:T(8,128)(2,1)} copy(bf16[16,32,8,256]{3,0,1,2:T(8,128)(2,1)S(1)} %fusion.10) | data formatting | bytes 4194304 | tf_op jit(solution)/shard_map/convert_element_type | solution.py:29
  141.1 4.2 %dot_general.24 = bf16[16,32,2048]{2,1,0:T(8,128)(2,1)} reshape(bf16[16,32,8,256]{3,2,1,0:T(8,128)(2,1)} %copy.27) | data formatting | bytes 4194304 | tf_op jit(solution)/shard_map/dot_general | solution.py:30
  145.3 14.4 %fusion.2 = f32[32,4096]{1,0:T(8,128)} fusion(bf16[16,32,4096]{2,1,0:T(8,128)(2,1)} %param.8, bf16[16,32,2048]{2,1,0:T(8,128)(2,1)} %dot_general.24, bf16[2048,4096]{1,0:T(8,128)(2,1)} %param.10), kind=kOutput, calls=%fused_computation.4 | convolution fusion | flops 8596094976 | bytes 23592960 | tf_op jit(solution)/shard_map/dot_general | solution.py:30
  159.8 0.0 all-gather.7.cloned.1.call-update
  159.8 0.0 all-to-all-done
  159.8 0.2 reduce_sum.39
  160.1 1.1 copy.32
  161.2 42.8 %all-gather.7.cloned.1.call-done = f32[128,4096]{1,0:T(8,128)} async-done(((f32[32,4096]{1,0:T(8,128)}), f32[128,4096]{1,0:T(8,128)}) %all-gather.7.cloned.1.call-update) | async-done | bytes 2097168 | tf_op jit(solution)/shard_map/all_gather | solution.py:34
  204.0 2.5 %reduce_sum.38 = f32[32,4096]{1,0:T(8,128)} reduce(f32[4,32,4096]{2,1,0:T(8,128)} %bitcast.46, f32[]{:T(128)} %constant.3.clone.1), dimensions={0}, to_apply=%region_2.0 | reduce | flops 393216 | bytes 2621444 | tf_op jit(solution)/shard_map/reduce_sum | solution.py:34
  (1 shorter events, 0.0 us)
Async XLA Ops:
  8.0 18.9 %copy-start = (bf16[16,32,256]{2,1,0:T(8,128)(2,1)S(1)}, bf16[16,32,256]{2,1,0:T(8,128)(2,1)}, u32[]{:S(2)}) copy-start(bf16[16,32,256]{2,1,0:T(8,128)(2,1)} %param.9) | copy-start | bytes 786436
  8.0 72.5 %reduce-scatter.2.cloned.1.call-start = ((), (), s32[]{:S(2)}) async-start(), calls=%async_computation.2 | async-start | bytes 4718592 | tf_op jit(solution)/shard_map/reduce_scatter | solution.py:39
  26.2 0.7 copy-start.3
  26.2 0.7 copy-start.4
  26.2 0.8 copy-start.1
  26.2 1.9 copy-start.2
  26.2 104.3 %all-gather.5.cloned.1.call-start = ((), (), s32[]{:S(2)}) async-start(), calls=%async_computation.3 | async-start | bytes 8650752 | tf_op jit(solution)/shard_map/all_gather | solution.py:21
  84.9 74.9 %all-to-all-start = ((f32[4,16,32,256]{3,1,2,0:T(8,128)}), f32[4,16,32,256]{3,1,2,0:T(8,128)S(1)}, u32[]{:S(2)}, u32[]{:S(2)}) async-start(f32[4,16,32,256]{3,1,2,0:T(8,128)} %copy.30), calls=%async_computation.1 | async-start | bytes 4194304 | tf_op jit(solution)/shard_map/all_to_all | solution.py:56
  89.5 114.5 %all-gather.7.cloned.1.call-start = ((), (), s32[]{:S(2)}) async-start(), calls=%async_computation.4 | async-start | bytes 2621440 | tf_op jit(solution)/shard_map/all_gather | solution.py:34
Sparse Core Ops, SparseCore 0:
  26.3 54.1 reduce-scatter.1
Sparse Core Ops, SparseCore 1:
  30.1 100.3 all-gather.4
  159.9 44.0 all-gather.6
